TPU v7x, 32 devices: a whole 2x2x4 slice. The times are simulated.
32 devices in a mesh: lat: 2 (over x), lon: 4 (over y, core), lev: 4 (over z).
Axes of the slice: x: 2, y: 2, z: 4, core: 2. Of those that a mesh axis runs over, the one named last changes fastest.
Arguments:
- initial_state: float32 [8, 384, 128, 128], P('lat', 'lon', 'lev'), may hold values from 0.5 to 2
- scaled_wind_north: float32 [8, 384, 128, 128], P('lat', 'lon', 'lev'), may hold values from -0.3 to 0.3
- scaled_wind_east: float32 [8, 384, 128, 128], P('lat', 'lon', 'lev'), may hold values from -0.3 to 0.3
- scaled_wind_upward: float32 [8, 384, 128, 128], P('lat', 'lon', 'lev'), may hold values from -0.3 to 0.3
Outputs:
- normalised_state: float32 [8, 384, 128, 128], P('lat', 'lon', 'lev')
- temperature_end: float32 [8, 384, 128, 128], P('lat', 'lon', 'lev')
All inputs are finite; a program needn't handle non-finite values.
Results may differ from a plain program's by a relative error of at most 0.00002.
Values sent between devices are 32-bit elements; how exact they have to be, the bound alone decides.
A program may use at most 128 MiB of HBM per device.

v0:
```python
import jax
import jax.numpy as jnp
from jax import lax
from jax.sharding import PartitionSpec as P

STEPS = 4


def with_halo(cells, sides, width):
    for axis, dim in sides:
        count = lax.axis_size(axis)
        ends = count - 1
        head = lax.slice_in_dim(cells, 0, width, axis=dim)
        tail = lax.slice_in_dim(cells, cells.shape[dim] - width, cells.shape[dim], axis=dim)
        cells = jnp.concatenate(
            [
                lax.ppermute(tail, axis, [(i, (i + 1) % count) for i in range(ends)]),
                cells,
                lax.ppermute(head, axis, [((i + 1) % count, i) for i in range(ends)]),
            ],
            axis=dim,
        )
    return cells


def strip_edges(values, dims):
    for dim in dims:
        values = lax.slice_in_dim(values, 1, values.shape[dim] - 1, axis=dim)
    return values


def neighbour(values, dim, start, dims):
    others = [other for other in dims if other != dim]
    values = strip_edges(values, others)
    return lax.slice_in_dim(values, start, start + values.shape[dim] - 2, axis=dim)


def march_one_step(padded_state, scaled_wind_north, scaled_wind_east, scaled_wind_upward):
    middle = strip_edges(padded_state, (0, 1, 2))
    lower = [neighbour(padded_state, dim, 0, (0, 1, 2)) for dim in (0, 1, 2)]
    upper = [neighbour(padded_state, dim, 2, (0, 1, 2)) for dim in (0, 1, 2)]
    slopes = [above - below for above, below in zip(upper, lower)]
    smooth_rate = 0.05
    spread = lower[0] + upper[0] + lower[1] + upper[1] + lower[2] + upper[2] - 6.0 * middle
    return (
        middle
        - scaled_wind_north * slopes[0]
        - scaled_wind_east * slopes[1]
        - scaled_wind_upward * slopes[2]
        + smooth_rate * spread
    )


def shards(initial_state, scaled_wind_north, scaled_wind_east, scaled_wind_upward):
    for step in range(STEPS):
        padded_state = with_halo(initial_state, (("lat", 0), ("lon", 1), ("lev", 2)), 1)
        initial_state = march_one_step(
            padded_state, scaled_wind_north, scaled_wind_east, scaled_wind_upward
        )
    number_of_values = initial_state.shape[1] * lax.axis_size("lon")
    guess = 1.0
    moved = initial_state - guess
    totals, squares = lax.psum(
        (jnp.sum(moved, axis=1, keepdims=True), jnp.sum(moved * moved, axis=1, keepdims=True)),
        "lon",
    )
    vertical_mean = guess + totals / number_of_values
    symmetric_slope = initial_state - vertical_mean
    line_variance = squares / number_of_values - totals / number_of_values * (
        totals / number_of_values
    )
    normalised_state = symmetric_slope * lax.rsqrt(line_variance + 0.0001)
    return (normalised_state, initial_state)


def solution(mesh):
    return jax.shard_map(
        shards,
        mesh=mesh,
        in_specs=(
            P("lat", "lon", "lev", None),
            P("lat", "lon", "lev", None),
            P("lat", "lon", "lev", None),
            P("lat", "lon", "lev", None),
        ),
        out_specs=(P("lat", "lon", "lev", None), P("lat", "lon", "lev", None)),
        check_vma=False,
    )
```

profile of v0, /device:TPU:0, one launch (start us, length us, event | category | flops | bytes accessed | tf_op | source)
XLA Modules:
  0.0 387.5 jit_solution(1042156766580561477)
XLA Ops:
  7.2 2.3 fusion.4
  9.6 5.1 %collective-permute-start.1 = (f32[1,96,32,128]{3,2,1,0:T(8,128)S(1)}, f32[1,96,32,128]{3,2,1,0:T(8,128)S(1)}, u32[]{:S(2)}, u32[]{:S(2)}) collective-permute-start(f32[1,96,32,128]{3,2,1,0:T(8,128)S(1)} %get-tuple-element.32), channel_id=1, source_target_pairs={{0,16},{1,17},{2,18},{3,19},{4,20},{5,21},{6,22},{7,23},{8,24},{9,... | collective-permute-start | bytes 4718600 | tf_op jit(solution)/shard_map/ppermute | solution.py:17
  14.7 1.3 collective-permute-start
  16.0 32.2 %collective-permute-done.1 = f32[1,96,32,128]{3,2,1,0:T(8,128)S(1)} collective-permute-done((f32[1,96,32,128]{3,2,1,0:T(8,128)S(1)}, f32[1,96,32,128]{3,2,1,0:T(8,128)S(1)}, u32[]{:S(2)}, u32[]{:S(2)}) %collective-permute-start.1) | collective-permute-done | bytes 1572896 | tf_op jit(solution)/shard_map/ppermute | solution.py:17
  48.2 1.1 copy-done.9
  49.5 0.7 constant_dynamic-update-slice_fusion.1
  50.2 2.2 collective-permute-done
  52.6 1.3 collective-permute-start.3
  53.9 1.3 collective-permute-start.2
  55.2 3.6 collective-permute-done.2
  58.8 0.4 pad_maximum_fusion.79
  59.3 1.3 collective-permute-start.4
  60.6 4.6 %collective-permute-start.5 = (f32[6,98,1,128]{3,1,2,0:T(8,128)S(1)}, f32[6,98,1,128]{3,1,2,0:T(8,128)S(1)}, u32[]{:S(2)}, u32[]{:S(2)}) collective-permute-start(f32[6,98,1,128]{3,1,2,0:T(8,128)S(1)} %copy.29), channel_id=1, source_target_pairs={{0,1},{1,2},{2,3},{4,5},{5,6},{6,7},{8,9},{9,10},{10,11},{12,13},{... | collective-permute-start | bytes 903176 | tf_op jit(solution)/shard_map/ppermute | solution.py:17
  65.2 4.1 %collective-permute-done.4 = f32[6,98,1,128]{3,1,2,0:T(8,128)S(1)} collective-permute-done((f32[6,98,1,128]{3,1,2,0:T(8,128)S(1)}, f32[6,98,1,128]{3,1,2,0:T(8,128)S(1)}, u32[]{:S(2)}, u32[]{:S(2)}) %collective-permute-start.4) | collective-permute-done | bytes 301088 | tf_op jit(solution)/shard_map/ppermute | solution.py:19
  69.3 0.3 copy.28
  69.7 1.5 collective-permute-done.5
  71.1 1.0 copy.30
  72.1 25.8 %multiply_add_fusion.3 = f32[4,96,32,128]{3,2,1,0:T(8,128)S(1)} fusion(f32[4,96,32,128]{3,2,1,0:T(8,128)} %param.4, f32[4,96,32,128]{3,2,1,0:T(8,128)} %param.7, f32[6,98,1,128]{3,2,1,0:T(1,128)S(1)} %copy.28, f32[6,1,32,128]{3,2,1,0:T(8,128)} %copy-done.12, f32[6,96,32,128]{3,2,1,0:T(8,128)} %copy-done.1, f32[6,1,32,128]{3,2,1,0:T(8,128)S(1)} %collective-permute-done.3, ...), kind=kLoop, calls=%fused_computation.69 | loop fusion | flops 44040192 | bytes 44838912 | tf_op jit(solution)/shard_map/add | solution.py:46
  98.2 2.3 collective-permute-start.7
  100.5 1.3 collective-permute-start.6
  101.8 32.2 %collective-permute-done.7 = f32[1,96,32,128]{3,2,1,0:T(8,128)S(1)} collective-permute-done((f32[1,96,32,128]{3,2,1,0:T(8,128)S(1)}, f32[1,96,32,128]{3,2,1,0:T(8,128)S(1)}, u32[]{:S(2)}, u32[]{:S(2)}) %collective-permute-start.7) | collective-permute-done | bytes 1572896 | tf_op jit(solution)/shard_map/ppermute | solution.py:17
  134.1 4.8 %collective-permute-done.6 = f32[1,96,32,128]{3,2,1,0:T(8,128)S(1)} collective-permute-done((f32[1,96,32,128]{3,2,1,0:T(8,128)S(1)}, f32[1,96,32,128]{3,2,1,0:T(8,128)S(1)}, u32[]{:S(2)}, u32[]{:S(2)}) %collective-permute-start.6) | collective-permute-done | bytes 1572896 | tf_op jit(solution)/shard_map/ppermute | solution.py:19
  138.9 2.6 collective-permute-start.9
  141.4 1.3 collective-permute-start.8
  142.8 1.9 collective-permute-done.8
  144.6 0.9 pad_maximum_fusion.74
  145.6 1.3 collective-permute-start.10
  146.9 5.2 %collective-permute-start.11 = (f32[6,98,1,128]{3,1,2,0:T(8,128)S(1)}, f32[6,98,1,128]{3,1,2,0:T(8,128)S(1)}, u32[]{:S(2)}, u32[]{:S(2)}) collective-permute-start(f32[6,98,1,128]{3,1,2,0:T(8,128)S(1)} %copy.33), channel_id=1, source_target_pairs={{0,1},{1,2},{2,3},{4,5},{5,6},{6,7},{8,9},{9,10},{10,11},{12,13},{... | collective-permute-start | bytes 903176 | tf_op jit(solution)/shard_map/ppermute | solution.py:17
  152.1 4.1 %collective-permute-done.10 = f32[6,98,1,128]{3,1,2,0:T(8,128)S(1)} collective-permute-done((f32[6,98,1,128]{3,1,2,0:T(8,128)S(1)}, f32[6,98,1,128]{3,1,2,0:T(8,128)S(1)}, u32[]{:S(2)}, u32[]{:S(2)}) %collective-permute-start.10) | collective-permute-done | bytes 301088 | tf_op jit(solution)/shard_map/ppermute | solution.py:19
  156.3 0.3 copy.32
  156.6 1.5 collective-permute-done.11
  158.0 1.0 copy.34
  159.1 14.1 %multiply_add_fusion.2 = f32[4,96,32,128]{3,2,1,0:T(8,128)S(1)} fusion(f32[4,96,32,128]{3,2,1,0:T(8,128)S(1)} %multiply_add_fusion.3, f32[4,96,32,128]{3,2,1,0:T(8,128)} %param.7, f32[6,98,1,128]{3,2,1,0:T(1,128)S(1)} %copy.32, f32[6,1,32,128]{3,2,1,0:T(8,128)} %copy-done.13, f32[1,96,32,128]{3,2,1,0:T(8,128)} %copy-done.7, f32[1,96,32,128]{3,2,1,0:T(8,128)} %copy-done.4, ...), kind=kLoop, calls=%fused_computation.68 | loop fusion | flops 56623104 | bytes 35401728 | tf_op jit(solution)/shard_map/add | solution.py:46
  173.5 1.8 collective-permute-start.13
  175.3 1.3 collective-permute-start.12
  176.6 32.4 %collective-permute-done.13 = f32[1,96,32,128]{3,2,1,0:T(8,128)S(1)} collective-permute-done((f32[1,96,32,128]{3,2,1,0:T(8,128)S(1)}, f32[1,96,32,128]{3,2,1,0:T(8,128)S(1)}, u32[]{:S(2)}, u32[]{:S(2)}) %collective-permute-start.13) | collective-permute-done | bytes 1572896 | tf_op jit(solution)/shard_map/ppermute | solution.py:17
  209.1 4.8 %collective-permute-done.12 = f32[1,96,32,128]{3,2,1,0:T(8,128)S(1)} collective-permute-done((f32[1,96,32,128]{3,2,1,0:T(8,128)S(1)}, f32[1,96,32,128]{3,2,1,0:T(8,128)S(1)}, u32[]{:S(2)}, u32[]{:S(2)}) %collective-permute-start.12) | collective-permute-done | bytes 1572896 | tf_op jit(solution)/shard_map/ppermute | solution.py:19
  213.9 2.4 collective-permute-start.15
  216.3 1.6 collective-permute-start.14
  217.9 1.9 collective-permute-done.14
  219.7 0.8 pad_maximum_fusion.69
  220.7 1.3 collective-permute-start.16
  222.0 5.0 %collective-permute-start.17 = (f32[6,98,1,128]{3,1,2,0:T(8,128)S(1)}, f32[6,98,1,128]{3,1,2,0:T(8,128)S(1)}, u32[]{:S(2)}, u32[]{:S(2)}) collective-permute-start(f32[6,98,1,128]{3,1,2,0:T(8,128)S(1)} %copy.37), channel_id=1, source_target_pairs={{0,1},{1,2},{2,3},{4,5},{5,6},{6,7},{8,9},{9,10},{10,11},{12,13},{... | collective-permute-start | bytes 903176 | tf_op jit(solution)/shard_map/ppermute | solution.py:17
  227.0 4.3 %collective-permute-done.16 = f32[6,98,1,128]{3,1,2,0:T(8,128)S(1)} collective-permute-done((f32[6,98,1,128]{3,1,2,0:T(8,128)S(1)}, f32[6,98,1,128]{3,1,2,0:T(8,128)S(1)}, u32[]{:S(2)}, u32[]{:S(2)}) %collective-permute-start.16) | collective-permute-done | bytes 301088 | tf_op jit(solution)/shard_map/ppermute | solution.py:19
  231.7 1.5 collective-permute-done.17
  233.1 1.0 copy.38
  234.2 26.7 %multiply_add_fusion.1 = f32[4,96,32,128]{3,2,1,0:T(8,128)S(1)} fusion(f32[4,96,32,128]{3,2,1,0:T(8,128)} %copy-done, f32[4,96,32,128]{3,2,1,0:T(8,128)S(1)} %bitcast.7, f32[6,98,1,128]{3,2,1,0:T(1,128)S(1)} %copy.36, f32[6,1,32,128]{3,2,1,0:T(8,128)} %copy-done.14, f32[1,96,32,128]{3,2,1,0:T(8,128)} %copy-done.8, f32[1,96,32,128]{3,2,1,0:T(8,128)} %copy-done.5, ...), kind=kLoop, calls=%fused_computation.67 | loop fusion | flops 56623104 | bytes 35401728 | tf_op jit(solution)/shard_map/add | solution.py:46
  261.2 1.8 collective-permute-start.19
  263.0 1.3 collective-permute-start.18
  264.3 32.4 %collective-permute-done.19 = f32[1,96,32,128]{3,2,1,0:T(8,128)S(1)} collective-permute-done((f32[1,96,32,128]{3,2,1,0:T(8,128)S(1)}, f32[1,96,32,128]{3,2,1,0:T(8,128)S(1)}, u32[]{:S(2)}, u32[]{:S(2)}) %collective-permute-start.19) | collective-permute-done | bytes 1572896 | tf_op jit(solution)/shard_map/ppermute | solution.py:17
  296.8 4.8 %collective-permute-done.18 = f32[1,96,32,128]{3,2,1,0:T(8,128)S(1)} collective-permute-done((f32[1,96,32,128]{3,2,1,0:T(8,128)S(1)}, f32[1,96,32,128]{3,2,1,0:T(8,128)S(1)}, u32[]{:S(2)}, u32[]{:S(2)}) %collective-permute-start.18) | collective-permute-done | bytes 1572896 | tf_op jit(solution)/shard_map/ppermute | solution.py:19
  301.6 2.4 collective-permute-start.21
  304.0 1.3 collective-permute-start.20
  305.3 1.9 collective-permute-done.20
  307.2 0.8 pad_maximum_fusion.68
  308.0 4.4 %collective-permute-start.23 = (f32[6,98,1,128]{3,1,2,0:T(8,128)S(1)}, f32[6,98,1,128]{3,1,2,0:T(8,128)S(1)}, u32[]{:S(2)}, u32[]{:S(2)}) collective-permute-start(f32[6,98,1,128]{3,1,2,0:T(8,128)S(1)} %copy.41), channel_id=1, source_target_pairs={{0,1},{1,2},{2,3},{4,5},{5,6},{6,7},{8,9},{9,10},{10,11},{12,13},{... | collective-permute-start | bytes 903176 | tf_op jit(solution)/shard_map/ppermute | solution.py:17
  312.5 1.5 collective-permute-start.22
  314.0 4.5 %collective-permute-done.23 = f32[6,98,1,128]{3,1,2,0:T(8,128)S(1)} collective-permute-done((f32[6,98,1,128]{3,1,2,0:T(8,128)S(1)}, f32[6,98,1,128]{3,1,2,0:T(8,128)S(1)}, u32[]{:S(2)}, u32[]{:S(2)}) %collective-permute-start.23) | collective-permute-done | bytes 301088 | tf_op jit(solution)/shard_map/ppermute | solution.py:17
  318.9 4.5 %collective-permute-done.22 = f32[6,98,1,128]{3,1,2,0:T(8,128)S(1)} collective-permute-done((f32[6,98,1,128]{3,1,2,0:T(8,128)S(1)}, f32[6,98,1,128]{3,1,2,0:T(8,128)S(1)}, u32[]{:S(2)}, u32[]{:S(2)}) %collective-permute-start.22) | collective-permute-done | bytes 301088 | tf_op jit(solution)/shard_map/ppermute | solution.py:19
  323.3 1.0 copy.40
  324.4 15.7 %add_reduce_fusion = (f32[4,32,128]{2,1,0:T(8,128)}, f32[4,32,128]{2,1,0:T(8,128)}, f32[4,96,32,128]{3,2,1,0:T(8,128)}) fusion(f32[4,96,32,128]{3,2,1,0:T(8,128)S(1)} %multiply_add_fusion.1, f32[4,96,32,128]{3,2,1,0:T(8,128)S(1)} %bitcast.7, f32[6,1,32,128]{3,2,1,0:T(8,128)} %copy-done.11, f32[1,96,32,128]{3,2,1,0:T(8,128)} %copy-done.6, ...), kind=kLoop, calls=%fused_computation.70 | loop fusion | flops 62881792 | bytes 35532800 | tf_op jit(solution)/shard_map/reduce_sum | solution.py:64
  340.1 33.0 %all-reduce.3.cloned.1.call-done = (f32[4,1,32,128]{3,2,0,1:T(8,128)}, f32[4,1,32,128]{3,2,0,1:T(8,128)}) async-done(((f32[4,1,32,128]{3,2,0,1:T(8,128)}, f32[4,1,32,128]{3,2,0,1:T(8,128)}), (f32[4,1,32,128]{3,2,0,1:T(8,128)}, f32[4,1,32,128]{3,2,0,1:T(8,128)})) %all-reduce.3.cloned.1.call-update) | async-done | bytes 131088 | tf_op jit(solution)/shard_map/psum | solution.py:63
  373.0 0.9 add_bitcast_fusion
  373.9 6.7 %subtract_multiply_fusion = f32[4,96,32,128]{3,2,1,0:T(8,128)} fusion(f32[4,96,32,128]{3,2,1,0:T(8,128)} %get-tuple-element.8, f32[4,32,128]{2,1,0:T(8,128)S(1)} %get-tuple-element.34, f32[4,32,128]{2,1,0:T(8,128)S(1)} %get-tuple-element.33), kind=kLoop, calls=%fused_computation.65 | loop fusion | flops 3145728 | bytes 12713984 | tf_op jit(solution)/shard_map/mul | solution.py:72
  (59 shorter events, 2.2 us)
Async XLA Ops:
  7.2 365.9 %all-reduce.3.cloned.1.call-start = ((), (), s32[]{:S(2)}) async-start(), calls=%async_computation | async-start | bytes 262144 | tf_op jit(solution)/shard_map/psum | solution.py:63
  7.2 42.3 %copy-start.2 = (f32[4,96,32,128]{3,2,1,0:T(8,128)S(1)}, f32[4,96,32,128]{3,2,1,0:T(8,128)}, u32[]{:S(2)}) copy-start(f32[4,96,32,128]{3,2,1,0:T(8,128)} %param.4) | copy-start | bytes 18874372
  9.6 38.6 %collective-permute-start.1 = (f32[1,96,32,128]{3,2,1,0:T(8,128)S(1)}, f32[1,96,32,128]{3,2,1,0:T(8,128)S(1)}, u32[]{:S(2)}, u32[]{:S(2)}) collective-permute-start(f32[1,96,32,128]{3,2,1,0:T(8,128)S(1)} %get-tuple-element.32), channel_id=1, source_target_pairs={{0,16},{1,17},{2,18},{3,19},{4,20},{5,21},{6,22},{7,23},{8,24},{9,... | collective-permute-start | bytes 4718600 | tf_op jit(solution)/shard_map/ppermute | solution.py:17
  14.7 37.7 %collective-permute-start = (f32[1,96,32,128]{3,2,1,0:T(8,128)S(1)}, f32[1,96,32,128]{3,2,1,0:T(8,128)S(1)}, u32[]{:S(2)}, u32[]{:S(2)}) collective-permute-start(f32[1,96,32,128]{3,2,1,0:T(8,128)S(1)} %get-tuple-element.31), channel_id=1, source_target_pairs={{16,0},{17,1},{18,2},{19,3},{20,4},{21,5},{22,6},{23,7},{24,8},{25... | collective-permute-start | bytes 4718600 | tf_op jit(solution)/shard_map/ppermute | solution.py:19
  48.2 1.1 copy-start.9
  52.4 6.8 %copy-start.10 = (f32[1,96,32,128]{3,2,1,0:T(8,128)}, f32[1,96,32,128]{3,2,1,0:T(8,128)S(1)}, u32[]{:S(2)}) copy-start(f32[1,96,32,128]{3,2,1,0:T(8,128)S(1)} %collective-permute-done) | copy-start | bytes 4718596
  52.6 18.5 %copy-start.1 = (f32[6,96,32,128]{3,2,1,0:T(8,128)}, f32[6,96,32,128]{3,2,1,0:T(8,128)S(1)}, u32[]{:S(2)}) copy-start(f32[6,96,32,128]{3,2,1,0:T(8,128)S(1)} %constant_dynamic-update-slice_fusion) | copy-start | bytes 28311556
  52.6 2.6 collective-permute-start.3
  53.9 4.9 %collective-permute-start.2 = (f32[6,1,32,128]{3,2,1,0:T(8,128)S(1)}, f32[6,1,32,128]{3,2,1,0:T(8,128)S(1)}, u32[]{:S(2)}, u32[]{:S(2)}) collective-permute-start(f32[6,1,32,128]{3,2,1,0:T(8,128)S(1)} %get-tuple-element.24), channel_id=1, source_target_pairs={{4,0},{8,4},{12,8},{5,1},{9,5},{13,9},{6,2},{10,6},{14,10},{7,3},{... | collective-permute-start | bytes 294920 | tf_op jit(solution)/shard_map/ppermute | solution.py:19
  58.8 12.3 %copy-start.12 = (f32[6,1,32,128]{3,2,1,0:T(8,128)}, f32[6,1,32,128]{3,2,1,0:T(8,128)S(1)}, u32[]{:S(2)}) copy-start(f32[6,1,32,128]{3,2,1,0:T(8,128)S(1)} %collective-permute-done.2) | copy-start | bytes 294916
  59.3 10.0 %collective-permute-start.4 = (f32[6,98,1,128]{3,1,2,0:T(8,128)S(1)}, f32[6,98,1,128]{3,1,2,0:T(8,128)S(1)}, u32[]{:S(2)}, u32[]{:S(2)}) collective-permute-start(f32[6,98,1,128]{3,1,2,0:T(8,128)S(1)} %copy.27), channel_id=1, source_target_pairs={{1,0},{2,1},{3,2},{5,4},{6,5},{7,6},{9,8},{10,9},{11,10},{13,12},{... | collective-permute-start | bytes 903176 | tf_op jit(solution)/shard_map/ppermute | solution.py:19
  60.6 10.5 %collective-permute-start.5 = (f32[6,98,1,128]{3,1,2,0:T(8,128)S(1)}, f32[6,98,1,128]{3,1,2,0:T(8,128)S(1)}, u32[]{:S(2)}, u32[]{:S(2)}) collective-permute-start(f32[6,98,1,128]{3,1,2,0:T(8,128)S(1)} %copy.29), channel_id=1, source_target_pairs={{0,1},{1,2},{2,3},{4,5},{5,6},{6,7},{8,9},{9,10},{10,11},{12,13},{... | collective-permute-start | bytes 903176 | tf_op jit(solution)/shard_map/ppermute | solution.py:17
  98.2 35.8 %collective-permute-start.7 = (f32[1,96,32,128]{3,2,1,0:T(8,128)S(1)}, f32[1,96,32,128]{3,2,1,0:T(8,128)S(1)}, u32[]{:S(2)}, u32[]{:S(2)}) collective-permute-start(f32[1,96,32,128]{3,2,1,0:T(8,128)S(1)} %get-tuple-element.29), channel_id=1, source_target_pairs={{0,16},{1,17},{2,18},{3,19},{4,20},{5,21},{6,22},{7,23},{8,24},{9,... | collective-permute-start | bytes 4718600 | tf_op jit(solution)/shard_map/ppermute | solution.py:17
  100.5 38.3 %collective-permute-start.6 = (f32[1,96,32,128]{3,2,1,0:T(8,128)S(1)}, f32[1,96,32,128]{3,2,1,0:T(8,128)S(1)}, u32[]{:S(2)}, u32[]{:S(2)}) collective-permute-start(f32[1,96,32,128]{3,2,1,0:T(8,128)S(1)} %get-tuple-element.30), channel_id=1, source_target_pairs={{16,0},{17,1},{18,2},{19,3},{20,4},{21,5},{22,6},{23,7},{24,8},{25... | collective-permute-start | bytes 4718600 | tf_op jit(solution)/shard_map/ppermute | solution.py:19
  134.1 11.5 %copy-start.4 = (f32[1,96,32,128]{3,2,1,0:T(8,128)}, f32[1,96,32,128]{3,2,1,0:T(8,128)S(1)}, u32[]{:S(2)}) copy-start(f32[1,96,32,128]{3,2,1,0:T(8,128)S(1)} %collective-permute-done.7) | copy-start | bytes 4718596
  138.8 6.7 %copy-start.7 = (f32[1,96,32,128]{3,2,1,0:T(8,128)}, f32[1,96,32,128]{3,2,1,0:T(8,128)S(1)}, u32[]{:S(2)}) copy-start(f32[1,96,32,128]{3,2,1,0:T(8,128)S(1)} %collective-permute-done.6) | copy-start | bytes 4718596
  138.9 3.9 %collective-permute-start.9 = (f32[6,1,32,128]{3,2,1,0:T(8,128)S(1)}, f32[6,1,32,128]{3,2,1,0:T(8,128)S(1)}, u32[]{:S(2)}, u32[]{:S(2)}) collective-permute-start(f32[6,1,32,128]{3,2,1,0:T(8,128)S(1)} %get-tuple-element.21), channel_id=1, source_target_pairs={{0,4},{4,8},{8,12},{1,5},{5,9},{9,13},{2,6},{6,10},{10,14},{3,7},{... | collective-permute-start | bytes 294920 | tf_op jit(solution)/shard_map/ppermute | solution.py:17
  141.4 3.2 collective-permute-start.8
  144.6 7.5 %copy-start.13 = (f32[6,1,32,128]{3,2,1,0:T(8,128)}, f32[6,1,32,128]{3,2,1,0:T(8,128)S(1)}, u32[]{:S(2)}) copy-start(f32[6,1,32,128]{3,2,1,0:T(8,128)S(1)} %collective-permute-done.8) | copy-start | bytes 294916
  145.6 10.7 %collective-permute-start.10 = (f32[6,98,1,128]{3,1,2,0:T(8,128)S(1)}, f32[6,98,1,128]{3,1,2,0:T(8,128)S(1)}, u32[]{:S(2)}, u32[]{:S(2)}) collective-permute-start(f32[6,98,1,128]{3,1,2,0:T(8,128)S(1)} %copy.31), channel_id=1, source_target_pairs={{1,0},{2,1},{3,2},{5,4},{6,5},{7,6},{9,8},{10,9},{11,10},{13,12},{... | collective-permute-start | bytes 903176 | tf_op jit(solution)/shard_map/ppermute | solution.py:19
  146.9 11.1 %collective-permute-start.11 = (f32[6,98,1,128]{3,1,2,0:T(8,128)S(1)}, f32[6,98,1,128]{3,1,2,0:T(8,128)S(1)}, u32[]{:S(2)}, u32[]{:S(2)}) collective-permute-start(f32[6,98,1,128]{3,1,2,0:T(8,128)S(1)} %copy.33), channel_id=1, source_target_pairs={{0,1},{1,2},{2,3},{4,5},{5,6},{6,7},{8,9},{9,10},{10,11},{12,13},{... | collective-permute-start | bytes 903176 | tf_op jit(solution)/shard_map/ppermute | solution.py:17
  173.2 46.6 %copy-start = (f32[4,96,32,128]{3,2,1,0:T(8,128)}, f32[4,96,32,128]{3,2,1,0:T(8,128)S(1)}, u32[]{:S(2)}) copy-start(f32[4,96,32,128]{3,2,1,0:T(8,128)S(1)} %multiply_add_fusion.2) | copy-start | bytes 18874372
  173.5 35.6 %collective-permute-start.13 = (f32[1,96,32,128]{3,2,1,0:T(8,128)S(1)}, f32[1,96,32,128]{3,2,1,0:T(8,128)S(1)}, u32[]{:S(2)}, u32[]{:S(2)}) collective-permute-start(f32[1,96,32,128]{3,2,1,0:T(8,128)S(1)} %get-tuple-element.27), channel_id=1, source_target_pairs={{0,16},{1,17},{2,18},{3,19},{4,20},{5,21},{6,22},{7,23},{8,24},{9,... | collective-permute-start | bytes 4718600 | tf_op jit(solution)/shard_map/ppermute | solution.py:17
  175.3 38.5 %collective-permute-start.12 = (f32[1,96,32,128]{3,2,1,0:T(8,128)S(1)}, f32[1,96,32,128]{3,2,1,0:T(8,128)S(1)}, u32[]{:S(2)}, u32[]{:S(2)}) collective-permute-start(f32[1,96,32,128]{3,2,1,0:T(8,128)S(1)} %get-tuple-element.28), channel_id=1, source_target_pairs={{16,0},{17,1},{18,2},{19,3},{20,4},{21,5},{22,6},{23,7},{24,8},{25... | collective-permute-start | bytes 4718600 | tf_op jit(solution)/shard_map/ppermute | solution.py:19
  209.1 11.5 %copy-start.5 = (f32[1,96,32,128]{3,2,1,0:T(8,128)}, f32[1,96,32,128]{3,2,1,0:T(8,128)S(1)}, u32[]{:S(2)}) copy-start(f32[1,96,32,128]{3,2,1,0:T(8,128)S(1)} %collective-permute-done.13) | copy-start | bytes 4718596
  213.9 6.8 %copy-start.8 = (f32[1,96,32,128]{3,2,1,0:T(8,128)}, f32[1,96,32,128]{3,2,1,0:T(8,128)S(1)}, u32[]{:S(2)}) copy-start(f32[1,96,32,128]{3,2,1,0:T(8,128)S(1)} %collective-permute-done.12) | copy-start | bytes 4718596
  213.9 4.0 %collective-permute-start.15 = (f32[6,1,32,128]{3,2,1,0:T(8,128)S(1)}, f32[6,1,32,128]{3,2,1,0:T(8,128)S(1)}, u32[]{:S(2)}, u32[]{:S(2)}) collective-permute-start(f32[6,1,32,128]{3,2,1,0:T(8,128)S(1)} %get-tuple-element.19), channel_id=1, source_target_pairs={{0,4},{4,8},{8,12},{1,5},{5,9},{9,13},{2,6},{6,10},{10,14},{3,7},{... | collective-permute-start | bytes 294920 | tf_op jit(solution)/shard_map/ppermute | solution.py:17
  216.3 17.9 %slice-start = ((s8[6291456]{0:T(1024)(128)(4,1)}), s8[4194304]{0:T(1024)(128)(4,1)S(1)}, s32[]{:S(2)}) async-start(s8[6291456]{0:T(1024)(128)(4,1)} %bitcast.6), calls=%async_computation.1 | async-start | bytes 8388608
  216.3 17.9 %slice-start.1 = ((s8[6291456]{0:T(1024)(128)(4,1)}), s8[2097152]{0:T(1024)(128)(4,1)S(1)}, s32[]{:S(2)}) async-start(s8[6291456]{0:T(1024)(128)(4,1)} %bitcast.6), calls=%async_computation.2 | async-start | bytes 4194304
  216.3 3.5 collective-permute-start.14
  219.7 7.3 %copy-start.14 = (f32[6,1,32,128]{3,2,1,0:T(8,128)}, f32[6,1,32,128]{3,2,1,0:T(8,128)S(1)}, u32[]{:S(2)}) copy-start(f32[6,1,32,128]{3,2,1,0:T(8,128)S(1)} %collective-permute-done.14) | copy-start | bytes 294916
  220.7 10.7 %collective-permute-start.16 = (f32[6,98,1,128]{3,1,2,0:T(8,128)S(1)}, f32[6,98,1,128]{3,1,2,0:T(8,128)S(1)}, u32[]{:S(2)}, u32[]{:S(2)}) collective-permute-start(f32[6,98,1,128]{3,1,2,0:T(8,128)S(1)} %copy.35), channel_id=1, source_target_pairs={{1,0},{2,1},{3,2},{5,4},{6,5},{7,6},{9,8},{10,9},{11,10},{13,12},{... | collective-permute-start | bytes 903176 | tf_op jit(solution)/shard_map/ppermute | solution.py:19
  222.0 11.1 %collective-permute-start.17 = (f32[6,98,1,128]{3,1,2,0:T(8,128)S(1)}, f32[6,98,1,128]{3,1,2,0:T(8,128)S(1)}, u32[]{:S(2)}, u32[]{:S(2)}) collective-permute-start(f32[6,98,1,128]{3,1,2,0:T(8,128)S(1)} %copy.37), channel_id=1, source_target_pairs={{0,1},{1,2},{2,3},{4,5},{5,6},{6,7},{8,9},{9,10},{10,11},{12,13},{... | collective-permute-start | bytes 903176 | tf_op jit(solution)/shard_map/ppermute | solution.py:17
  261.2 35.6 %collective-permute-start.19 = (f32[1,96,32,128]{3,2,1,0:T(8,128)S(1)}, f32[1,96,32,128]{3,2,1,0:T(8,128)S(1)}, u32[]{:S(2)}, u32[]{:S(2)}) collective-permute-start(f32[1,96,32,128]{3,2,1,0:T(8,128)S(1)} %get-tuple-element.25), channel_id=1, source_target_pairs={{0,16},{1,17},{2,18},{3,19},{4,20},{5,21},{6,22},{7,23},{8,24},{9,... | collective-permute-start | bytes 4718600 | tf_op jit(solution)/shard_map/ppermute | solution.py:17
  263.0 38.5 %collective-permute-start.18 = (f32[1,96,32,128]{3,2,1,0:T(8,128)S(1)}, f32[1,96,32,128]{3,2,1,0:T(8,128)S(1)}, u32[]{:S(2)}, u32[]{:S(2)}) collective-permute-start(f32[1,96,32,128]{3,2,1,0:T(8,128)S(1)} %get-tuple-element.26), channel_id=1, source_target_pairs={{16,0},{17,1},{18,2},{19,3},{20,4},{21,5},{22,6},{23,7},{24,8},{25... | collective-permute-start | bytes 4718600 | tf_op jit(solution)/shard_map/ppermute | solution.py:19
  296.8 11.2 %copy-start.3 = (f32[1,96,32,128]{3,2,1,0:T(8,128)}, f32[1,96,32,128]{3,2,1,0:T(8,128)S(1)}, u32[]{:S(2)}) copy-start(f32[1,96,32,128]{3,2,1,0:T(8,128)S(1)} %collective-permute-done.19) | copy-start | bytes 4718596
  301.6 6.5 %copy-start.6 = (f32[1,96,32,128]{3,2,1,0:T(8,128)}, f32[1,96,32,128]{3,2,1,0:T(8,128)S(1)}, u32[]{:S(2)}) copy-start(f32[1,96,32,128]{3,2,1,0:T(8,128)S(1)} %collective-permute-done.18) | copy-start | bytes 4718596
  301.6 3.7 collective-permute-start.21
  304.0 3.2 collective-permute-start.20
  307.2 6.8 %copy-start.11 = (f32[6,1,32,128]{3,2,1,0:T(8,128)}, f32[6,1,32,128]{3,2,1,0:T(8,128)S(1)}, u32[]{:S(2)}) copy-start(f32[6,1,32,128]{3,2,1,0:T(8,128)S(1)} %collective-permute-done.20) | copy-start | bytes 294916
  308.0 10.5 %collective-permute-start.23 = (f32[6,98,1,128]{3,1,2,0:T(8,128)S(1)}, f32[6,98,1,128]{3,1,2,0:T(8,128)S(1)}, u32[]{:S(2)}, u32[]{:S(2)}) collective-permute-start(f32[6,98,1,128]{3,1,2,0:T(8,128)S(1)} %copy.41), channel_id=1, source_target_pairs={{0,1},{1,2},{2,3},{4,5},{5,6},{6,7},{8,9},{9,10},{10,11},{12,13},{... | collective-permute-start | bytes 903176 | tf_op jit(solution)/shard_map/ppermute | solution.py:17
  312.5 10.9 %collective-permute-start.22 = (f32[6,98,1,128]{3,1,2,0:T(8,128)S(1)}, f32[6,98,1,128]{3,1,2,0:T(8,128)S(1)}, u32[]{:S(2)}, u32[]{:S(2)}) collective-permute-start(f32[6,98,1,128]{3,1,2,0:T(8,128)S(1)} %copy.39), channel_id=1, source_target_pairs={{1,0},{2,1},{3,2},{5,4},{6,5},{7,6},{9,8},{10,9},{11,10},{13,12},{... | collective-permute-start | bytes 903176 | tf_op jit(solution)/shard_map/ppermute | solution.py:19
Sparse Core Ops, SparseCore 0:
  340.2 32.8 all-reduce.2
where the time goes:
time: 388 us
  waiting for transfers between devices  214 us (55%)
  other arithmetic  92.8 us (24%)
  starting transfers between devices  55 us (14%)
  between operations  14.6 us (4%)
  local copies, waits for them, and re-layouts  11 us (3%)
    ppermute x12, waiting for transfers between devices, with_halo(): lax.ppermute(tail, axis, [(i, (i + 1) % count) for i in range(ends)])  138 us
    add x3, other arithmetic, march_one_step(): middle - scaled_wind_north * slopes[0] - scaled_wind_east * slopes[1]  66.6 us
    ppermute x12, waiting for transfers between devices, with_halo(): lax.ppermute(head, axis, [((i + 1) % count, i) for i in range(ends)])  42.9 us
    ppermute x12, starting transfers between devices, with_halo(): lax.ppermute(tail, axis, [(i, (i + 1) % count) for i in range(ends)])  39 us
    psum x1, waiting for transfers between devices, shards(): lax.psum((jnp.sum(moved, axis=1, keepdims=True), jnp.sum(moved * moved, a...  33 us
    ppermute x12, starting transfers between devices, with_halo(): lax.ppermute(head, axis, [((i + 1) % count, i) for i in range(ends)])  16 us
    reduce_sum x1, other arithmetic, shards(): jnp.sum(moved, axis=1, keepdims=True)  15.7 us
  transfers between devices with their start and end apart: 25, of which 21 were waited for; matrix products, arithmetic and copies ran while one was open for 1% of the time, Pallas kernels for 0%

commit v1 on v0

v1 whole, which is shorter than its diff:
```python
import functools

import jax
import jax.numpy as jnp
from jax import lax
from jax.experimental import pallas as pl
from jax.experimental.pallas import tpu as pltpu
from jax.sharding import PartitionSpec as P

STEPS = 4
RATE = 0.05
EPS = 0.0001
MESH = pl.DeviceIdType.MESH
MIB = 1024 * 1024


def pieces_of(cells):
    return max(d for d in range(1, 9) if cells % d == 0)


def march_kernel(
    pieces, state_hbm, north_hbm, east_hbm, up_hbm, out_ref, stat_ref,
    cells, winds, lev_out, lev_in, stat_in,
    load_sem, lat_send, lat_recv, lon_send, lon_recv, lev_send, lev_recv, stat_send, stat_recv,
):
    rows, width, depth, members = out_ref.shape
    piece = width // pieces
    lat, lon, lev = lax.axis_index("lat"), lax.axis_index("lon"), lax.axis_index("lev")
    lats, lons, levs = lax.axis_size("lat"), lax.axis_size("lon"), lax.axis_size("lev")
    has_lat = (lat > 0, lat < lats - 1)
    has_lon = (lon > 0, lon < lons - 1)
    has_lev = (lev > 0, lev < levs - 1)
    lat_peer = (jnp.maximum(lat - 1, 0), jnp.minimum(lat + 1, lats - 1))
    lon_peer = (jnp.maximum(lon - 1, 0), jnp.minimum(lon + 1, lons - 1))
    lev_peer = (jnp.maximum(lev - 1, 0), jnp.minimum(lev + 1, levs - 1))

    loads = [
        pltpu.make_async_copy(
            state_hbm, cells.at[0, pl.ds(1, rows), pl.ds(1, width)], load_sem.at[0]
        )
    ]
    for k, ref in enumerate((north_hbm, east_hbm, up_hbm)):
        loads.append(pltpu.make_async_copy(ref, winds.at[k], load_sem.at[k + 1]))
    for load in loads:
        load.start()

    barrier = pltpu.get_barrier_semaphore()
    arrivals = lons - 1
    for axis, has, peer in (("lat", has_lat, lat_peer), ("lev", has_lev, lev_peer)):
        for side in (0, 1):
            arrivals = arrivals + has[side].astype(jnp.int32)

            @pl.when(has[side])
            def _(axis=axis, target=peer[side]):
                pl.semaphore_signal(barrier, inc=1, device_id={axis: target}, device_id_type=MESH)

    for k in range(1, lons):
        pl.semaphore_signal(
            barrier, inc=1, device_id={"lon": lax.rem(lon + k, lons)}, device_id_type=MESH
        )
    pl.semaphore_wait(barrier, arrivals)

    def lat_copy(parity, side, c, from_hbm=False):
        span = pl.ds(c * piece, piece)
        padded = pl.ds(1 + c * piece, piece)
        row = 0 if side == 0 else rows - 1
        src = state_hbm.at[row, span] if from_hbm else cells.at[parity, row + 1, padded]
        return pltpu.make_async_remote_copy(
            src_ref=src,
            dst_ref=cells.at[parity, rows + 1 if side == 0 else 0, padded],
            send_sem=lat_send.at[parity, side, c],
            recv_sem=lat_recv.at[parity, 1 - side, c],
            device_id={"lat": lat_peer[side]},
            device_id_type=MESH,
        )

    def lat_arrival(parity, side, c):
        here = cells.at[parity, 0 if side == 0 else rows + 1, pl.ds(1 + c * piece, piece)]
        return pltpu.make_async_remote_copy(
            src_ref=here, dst_ref=here,
            send_sem=lat_send.at[parity, side, c], recv_sem=lat_recv.at[parity, side, c],
            device_id={"lat": lat_peer[side]}, device_id_type=MESH,
        )

    def lon_copy(parity, side, from_hbm=False):
        col = 0 if side == 0 else width - 1
        mine = pl.ds(1, rows)
        src = state_hbm.at[:, col] if from_hbm else cells.at[parity, mine, col + 1]
        return pltpu.make_async_remote_copy(
            src_ref=src,
            dst_ref=cells.at[parity, mine, width + 1 if side == 0 else 0],
            send_sem=lon_send.at[parity, side],
            recv_sem=lon_recv.at[parity, 1 - side],
            device_id={"lon": lon_peer[side]},
            device_id_type=MESH,
        )

    def lon_arrival(parity, side):
        here = cells.at[parity, pl.ds(1, rows), 0 if side == 0 else width + 1]
        return pltpu.make_async_remote_copy(
            src_ref=here, dst_ref=here,
            send_sem=lon_send.at[parity, side], recv_sem=lon_recv.at[parity, side],
            device_id={"lon": lon_peer[side]}, device_id_type=MESH,
        )

    def lev_copy(parity, side):
        return pltpu.make_async_remote_copy(
            src_ref=lev_out.at[parity, side],
            dst_ref=lev_in.at[parity, 1 - side],
            send_sem=lev_send.at[parity, side],
            recv_sem=lev_recv.at[parity, 1 - side],
            device_id={"lev": lev_peer[side]},
            device_id_type=MESH,
        )

    def lev_arrival(parity, side):
        here = lev_in.at[parity, side]
        return pltpu.make_async_remote_copy(
            src_ref=here, dst_ref=here,
            send_sem=lev_send.at[parity, side], recv_sem=lev_recv.at[parity, side],
            device_id={"lev": lev_peer[side]}, device_id_type=MESH,
        )

    def each_side(has, act):
        for side in (0, 1):
            @pl.when(has[side])
            def _(side=side):
                act(side)

    def first_sends(c, carry):
        each_side(has_lat, lambda side: lat_copy(0, side, c, True).start())
        return carry

    lax.fori_loop(0, pieces, first_sends, 0)
    each_side(has_lon, lambda side: lon_copy(0, side, True).start())

    for side in (0, 1):
        @pl.when(jnp.logical_not(has_lat[side]))
        def _(row=0 if side == 0 else rows + 1):
            def clear(x, carry):
                for parity in (0, 1):
                    cells[parity, row, x + 1] = jnp.zeros((depth, members), jnp.float32)
                return carry

            lax.fori_loop(0, width, clear, 0)

        @pl.when(jnp.logical_not(has_lon[side]))
        def _(col=0 if side == 0 else width + 1):
            for parity in (0, 1):
                for y in range(rows):
                    cells[parity, y + 1, col] = jnp.zeros((depth, members), jnp.float32)

        @pl.when(jnp.logical_not(has_lev[side]))
        def _(side=side):
            def clear(x, carry):
                for parity in (0, 1):
                    for y in range(rows):
                        lev_in[parity, side, y, x] = jnp.zeros((1, members), jnp.float32)
                return carry

            lax.fori_loop(0, width, clear, 0)

    loads[0].wait()

    def first_levels(x, carry):
        for y in range(rows):
            lev_out[0, 0, y, x] = cells[0, y + 1, x + 1, 0:1, :]
            lev_out[0, 1, y, x] = cells[0, y + 1, x + 1, depth - 1 : depth, :]
        return carry

    lax.fori_loop(0, width, first_levels, 0)
    each_side(has_lev, lambda side: lev_copy(0, side).start())
    for load in loads[1:]:
        load.wait()

    level = lax.broadcasted_iota(jnp.int32, (depth, members), 0)
    bottom, top = level == 0, level == depth - 1

    def advance(parity, y, x):
        mid = cells[parity, y + 1, x + 1]
        south, north = cells[parity, y, x + 1], cells[parity, y + 2, x + 1]
        west, east = cells[parity, y + 1, x], cells[parity, y + 1, x + 2]
        below = jnp.where(bottom, lev_in[parity, 0, y, x], pltpu.roll(mid, 1, 0))
        above = jnp.where(top, lev_in[parity, 1, y, x], pltpu.roll(mid, depth - 1, 0))
        spread = (south + north) + (west + east) + (below + above) - 6.0 * mid
        return (
            mid
            - winds[0, y, x] * (north - south)
            - winds[1, y, x] * (east - west)
            - winds[2, y, x] * (above - below)
            + RATE * spread
        )

    for t in range(STEPS - 1):
        now, later = t % 2, (t + 1) % 2
        each_side(has_lev, lambda side: lev_arrival(now, side).wait_recv())
        each_side(has_lon, lambda side: lon_arrival(now, side).wait_recv())
        if t >= 1:
            each_side(has_lev, lambda side: lev_copy(later, side).wait_send())
            each_side(has_lon, lambda side: lon_copy(later, side, t == 1).wait_send())

        def one_piece(c, carry):
            each_side(has_lat, lambda side: lat_arrival(now, side, c).wait_recv())
            if t >= 1:
                each_side(has_lat, lambda side: lat_copy(later, side, c, t == 1).wait_send())

            def one_column(i, carry):
                x = c * piece + i
                for y in range(rows):
                    value = advance(now, y, x)
                    cells[later, y + 1, x + 1] = value
                    lev_out[later, 0, y, x] = value[0:1, :]
                    lev_out[later, 1, y, x] = value[depth - 1 : depth, :]
                return carry

            lax.fori_loop(0, piece, one_column, 0)
            each_side(has_lat, lambda side: lat_copy(later, side, c).start())
            return carry

        lax.fori_loop(0, pieces, one_piece, 0)
        each_side(has_lev, lambda side: lev_copy(later, side).start())
        each_side(has_lon, lambda side: lon_copy(later, side).start())

    now, later = (STEPS - 1) % 2, STEPS % 2
    each_side(has_lev, lambda side: lev_arrival(now, side).wait_recv())
    each_side(has_lon, lambda side: lon_arrival(now, side).wait_recv())

    def last_columns(y, start, count):
        def one_column(i, carry):
            out_ref[y, start + i] = advance(now, y, start + i)
            return carry

        lax.fori_loop(0, count, one_column, 0)

    def stat_copy(y, k):
        return pltpu.make_async_remote_copy(
            src_ref=stat_in.at[0, y],
            dst_ref=stat_in.at[k, y],
            send_sem=stat_send.at[y, k],
            recv_sem=stat_recv.at[y, k],
            device_id={"lon": lax.rem(lon + k, lons)},
            device_id_type=MESH,
        )

    def send_stats(y):
        zero = jnp.zeros((depth, members), jnp.float32)
        mean = lax.fori_loop(0, width, lambda x, s: s + out_ref[y, x], zero) / width

        def square(x, s):
            d = out_ref[y, x] - mean
            return s + d * d

        stat_in[0, y, 0] = mean
        stat_in[0, y, 1] = lax.fori_loop(0, width, square, zero)
        for k in range(1, lons):
            stat_copy(y, k).start()

    def take_stats(y):
        for k in range(1, lons):
            stat_copy(y, k).wait()
        means = [stat_in[k, y, 0] for k in range(lons)]
        mean = functools.reduce(jnp.add, means) / lons
        squares = functools.reduce(jnp.add, [stat_in[k, y, 1] for k in range(lons)])
        apart = functools.reduce(jnp.add, [(m - mean) * (m - mean) for m in means])
        variance = squares / (width * lons) + apart / lons
        stat_ref[y, 0] = mean
        stat_ref[y, 1] = lax.rsqrt(variance + EPS)

    low = has_lat[0].astype(jnp.int32)
    high = rows - has_lat[1].astype(jnp.int32)

    def free_row(y, carry):
        last_columns(y, 0, width)
        send_stats(y)
        return carry

    lax.fori_loop(low, high, free_row, 0)

    def last_piece(c, carry):
        def finish(side):
            lat_arrival(now, side, c).wait_recv()
            lat_copy(later, side, c).wait_send()
            last_columns(0 if side == 0 else rows - 1, c * piece, piece)

        each_side(has_lat, finish)
        return carry

    lax.fori_loop(0, pieces, last_piece, 0)
    each_side(has_lat, lambda side: send_stats(0 if side == 0 else rows - 1))

    def take(y, carry):
        take_stats(y)
        return carry

    lax.fori_loop(low, high, take, 0)
    each_side(has_lat, lambda side: take_stats(0 if side == 0 else rows - 1))

    for parity in (0, 1):
        each_side(has_lev, lambda side: lev_copy(parity, side).wait_send())
        each_side(has_lon, lambda side: lon_copy(parity, side).wait_send())

    def drain(c, carry):
        each_side(has_lat, lambda side: lat_copy(now, side, c).wait_send())
        return carry

    lax.fori_loop(0, pieces, drain, 0)


def finish_kernel(state_ref, stat_ref, norm_hbm, temp_hbm, staged, norm_sem, temp_sem):
    rows, width = state_ref.shape[:2]
    temp = pltpu.make_async_copy(state_ref, temp_hbm, temp_sem)
    temp.start()
    for y in range(rows):
        mean, scale = stat_ref[y, 0], stat_ref[y, 1]

        def one_column(x, carry):
            staged[y, x] = (state_ref[y, x] - mean) * scale
            return carry

        lax.fori_loop(0, width, one_column, 0, unroll=4)
        pltpu.make_async_copy(staged.at[y], norm_hbm.at[y], norm_sem.at[y]).start()
    for y in range(rows):
        pltpu.make_async_copy(staged.at[y], norm_hbm.at[y], norm_sem.at[y]).wait()
    temp.wait()


def solution(mesh):
    lons = mesh.shape["lon"]

    def shards(initial_state, scaled_wind_north, scaled_wind_east, scaled_wind_upward):
        rows, width, depth, members = initial_state.shape
        pieces = pieces_of(width)
        f32 = jnp.float32
        dma = pltpu.SemaphoreType.DMA
        anywhere = pl.BlockSpec(memory_space=pl.ANY)
        inside = pl.BlockSpec(memory_space=pltpu.VMEM)
        state, stats = pl.pallas_call(
            functools.partial(march_kernel, pieces),
            out_shape=(
                pltpu.VMEM((rows, width, depth, members), f32),
                pltpu.VMEM((rows, 2, depth, members), f32),
            ),
            in_specs=[anywhere] * 4,
            out_specs=(inside, inside),
            scratch_shapes=[
                pltpu.VMEM((2, rows + 2, width + 2, depth, members), f32),
                pltpu.VMEM((3, rows, width, depth, members), f32),
                pltpu.VMEM((2, 2, rows, width, 1, members), f32),
                pltpu.VMEM((2, 2, rows, width, 1, members), f32),
                pltpu.VMEM((lons, rows, 2, depth, members), f32),
                dma((4,)),
                dma((2, 2, pieces)),
                dma((2, 2, pieces)),
                dma((2, 2)),
                dma((2, 2)),
                dma((2, 2)),
                dma((2, 2)),
                dma((rows, lons)),
                dma((rows, lons)),
            ],
            compiler_params=pltpu.CompilerParams(
                collective_id=0, has_side_effects=True, vmem_limit_bytes=44 * MIB
            ),
            name="march",
        )(initial_state, scaled_wind_north, scaled_wind_east, scaled_wind_upward)
        return pl.pallas_call(
            finish_kernel,
            out_shape=(jax.ShapeDtypeStruct((rows, width, depth, members), f32),) * 2,
            in_specs=[inside, inside],
            out_specs=(anywhere, anywhere),
            scratch_shapes=[
                pltpu.VMEM((rows, width, depth, members), f32),
                dma((rows,)),
                dma,
            ],
            compiler_params=pltpu.CompilerParams(vmem_limit_bytes=16 * MIB),
            name="finish",
        )(state, stats)

    spec = P("lat", "lon", "lev", None)
    return jax.shard_map(
        shards,
        mesh=mesh,
        in_specs=(spec,) * 4,
        out_specs=(spec, spec),
        check_vma=False,
    )
```

time: 388 us -> 152 us (0.39)
  waiting for transfers between devices: 214 us -> 0 us
  Pallas kernels: 0 us -> 151 us
  other arithmetic: 92.8 us -> 0 us
  starting transfers between devices: 55 us -> 0 us
  between operations: 14.6 us -> 0.64 us
  local copies, waits for them, and re-layouts: 11 us -> 0 us
    ppermute x24 -> x0, waiting for transfers between devices: 181 us -> none  [the longest x12 138 us: with_halo(): lax.ppermute(tail, axis, [(i, (i + 1) % count) for i in range(ends)])]
    pallas_call x0 -> x2, Pallas kernels: none -> 151 us  [the longest x1 146 us: shards(): pl.pallas_call(functools.partial(march_kernel, pieces), out_shape=(pltpu....]
    add x3 -> x0, other arithmetic: 66.6 us -> none  [march_one_step(): middle - scaled_wind_north * slopes[0] - scaled_wind_east * slopes[1]]
    ppermute x24 -> x0, starting transfers between devices: 54.9 us -> none  [the longest x12 39 us: with_halo(): lax.ppermute(tail, axis, [(i, (i + 1) % count) for i in range(ends)])]
    psum x1 -> x0, waiting for transfers between devices: 33 us -> none  [shards(): lax.psum((jnp.sum(moved, axis=1, keepdims=True), jnp.sum(moved * moved, a...]
    reduce_sum x1 -> x0, other arithmetic: 15.7 us -> none  [shards(): jnp.sum(moved, axis=1, keepdims=True)]
    mul x1 -> x0, other arithmetic: 6.72 us -> none  [shards(): normalised_state = symmetric_slope * lax.rsqrt(line_variance + 0.0001)]
    ppermute x8 -> x0, local copies, waits for them, and re-layouts: 5.34 us -> none  [the longest x4 3.38 us: with_halo(): lax.ppermute(tail, axis, [(i, (i + 1) % count) for i in range(ends)])]
  transfers between devices with their start and end apart: 25 -> 0, of which waited for: 21 -> 0; matrix products, arithmetic and copies ran while one was open for 1% -> 0% of each run, Pallas kernels for 0% -> 0%
where the time goes in v1:
time: 152 us
  Pallas kernels  151 us (99%)
    pallas_call x1, Pallas kernels, shards(): pl.pallas_call(functools.partial(march_kernel, pieces), out_shape=(pltpu....  146 us
    pallas_call x1, Pallas kernels, shards(): pl.pallas_call(finish_kernel, out_shape=(jax.ShapeDtypeStruct((rows, widt...  4.68 us

profile of v1, /device:TPU:0, one launch (start us, length us, event | category | flops | bytes accessed | tf_op | source)
XLA Modules:
  0.0 151.6 jit_solution(4737229748883685968)
XLA Ops:
  0.6 146.3 %march.1 = (f32[4,96,32,128]{3,2,1,0:T(8,128)S(1)}, f32[4,2,32,128]{3,2,1,0:T(8,128)S(1)}) custom-call(f32[4,96,32,128]{3,2,1,0:T(8,128)} %state_hbm.1, f32[4,96,32,128]{3,2,1,0:T(8,128)} %north_hbm.1, f32[4,96,32,128]{3,2,1,0:T(8,128)} %east_hbm.1, f32[4,96,32,128]{3,2,1,0:T(8,128)} %up_hbm.1), custom_call_target="tpu_custom_call" | custom-call | tf_op jit(solution)/shard_map/march/pallas_call | solution.py:337
  146.9 4.7 %finish.1 = (f32[4,96,32,128]{3,2,1,0:T(8,128)}, f32[4,96,32,128]{3,2,1,0:T(8,128)}) custom-call(f32[4,96,32,128]{3,2,1,0:T(8,128)S(1)} %get-tuple-element.4.state_ref, f32[4,2,32,128]{3,2,1,0:T(8,128)S(1)} %get-tuple-element.5.stat_ref), custom_call_target="tpu_custom_call" | custom-call | tf_op jit(solution)/shard_map/finish/pallas_call | solution.py:366

commit v2 on v1

--- a/solution.py
+++ b/solution.py
@@ -20,11 +20,14 @@
 
 def march_kernel(
     pieces, state_hbm, north_hbm, east_hbm, up_hbm, out_ref, stat_ref,
-    cells, winds, lev_out, lev_in, stat_in,
-    load_sem, lat_send, lat_recv, lon_send, lon_recv, lev_send, lev_recv, stat_send, stat_recv,
+    cells, winds, lev_out, lev_in, stat_in, sums,
+    load_sem, lat_send, lat_recv, tile_send, tile_recv,
+    lon_send, lon_recv, lev_send, lev_recv, stat_send, stat_recv,
 ):
     rows, width, depth, members = out_ref.shape
+    tiles, tile = stat_in.shape[2], stat_in.shape[4]
     piece = width // pieces
+    head = max(pieces - 2, 0)
     lat, lon, lev = lax.axis_index("lat"), lax.axis_index("lon"), lax.axis_index("lev")
     lats, lons, levs = lax.axis_size("lat"), lax.axis_size("lon"), lax.axis_size("lev")
     has_lat = (lat > 0, lat < lats - 1)
@@ -41,8 +44,7 @@
     ]
     for k, ref in enumerate((north_hbm, east_hbm, up_hbm)):
         loads.append(pltpu.make_async_copy(ref, winds.at[k], load_sem.at[k + 1]))
-    for load in loads:
-        load.start()
+    loads[0].start()
 
     barrier = pltpu.get_barrier_semaphore()
     arrivals = lons - 1
@@ -82,6 +84,27 @@
             device_id={"lat": lat_peer[side]}, device_id_type=MESH,
         )
 
+    def tile_copy(parity, side, k):
+        span = pl.ds(1 + head * piece, width - head * piece)
+        levels = pl.ds(k * tile, tile)
+        return pltpu.make_async_remote_copy(
+            src_ref=cells.at[parity, 1 if side == 0 else rows, span, levels],
+            dst_ref=cells.at[parity, rows + 1 if side == 0 else 0, span, levels],
+            send_sem=tile_send.at[side, k],
+            recv_sem=tile_recv.at[1 - side, k],
+            device_id={"lat": lat_peer[side]},
+            device_id_type=MESH,
+        )
+
+    def tile_arrival(parity, side, k):
+        span = pl.ds(1 + head * piece, width - head * piece)
+        here = cells.at[parity, 0 if side == 0 else rows + 1, span, pl.ds(k * tile, tile)]
+        return pltpu.make_async_remote_copy(
+            src_ref=here, dst_ref=here,
+            send_sem=tile_send.at[side, k], recv_sem=tile_recv.at[side, k],
+            device_id={"lat": lat_peer[side]}, device_id_type=MESH,
+        )
+
     def lon_copy(parity, side, from_hbm=False):
         col = 0 if side == 0 else width - 1
         mine = pl.ds(1, rows)
@@ -133,6 +156,8 @@
 
     lax.fori_loop(0, pieces, first_sends, 0)
     each_side(has_lon, lambda side: lon_copy(0, side, True).start())
+    for load in loads[1:]:
+        load.start()
 
     for side in (0, 1):
         @pl.when(jnp.logical_not(has_lat[side]))
@@ -176,23 +201,25 @@
     level = lax.broadcasted_iota(jnp.int32, (depth, members), 0)
     bottom, top = level == 0, level == depth - 1
 
-    def advance(parity, y, x):
-        mid = cells[parity, y + 1, x + 1]
-        south, north = cells[parity, y, x + 1], cells[parity, y + 2, x + 1]
-        west, east = cells[parity, y + 1, x], cells[parity, y + 1, x + 2]
-        below = jnp.where(bottom, lev_in[parity, 0, y, x], pltpu.roll(mid, 1, 0))
-        above = jnp.where(top, lev_in[parity, 1, y, x], pltpu.roll(mid, depth - 1, 0))
+    def advance(parity, y, x, z=slice(None)):
+        whole = cells[parity, y + 1, x + 1]
+        mid = whole[z]
+        south, north = cells[parity, y, x + 1, z], cells[parity, y + 2, x + 1, z]
+        west, east = cells[parity, y + 1, x, z], cells[parity, y + 1, x + 2, z]
+        below = jnp.where(bottom, lev_in[parity, 0, y, x], pltpu.roll(whole, 1, 0))[z]
+        above = jnp.where(top, lev_in[parity, 1, y, x], pltpu.roll(whole, depth - 1, 0))[z]
         spread = (south + north) + (west + east) + (below + above) - 6.0 * mid
         return (
             mid
-            - winds[0, y, x] * (north - south)
-            - winds[1, y, x] * (east - west)
-            - winds[2, y, x] * (above - below)
+            - winds[0, y, x, z] * (north - south)
+            - winds[1, y, x, z] * (east - west)
+            - winds[2, y, x, z] * (above - below)
             + RATE * spread
         )
 
     for t in range(STEPS - 1):
         now, later = t % 2, (t + 1) % 2
+        whole_pieces = head if t == STEPS - 2 else pieces
         each_side(has_lev, lambda side: lev_arrival(now, side).wait_recv())
         each_side(has_lon, lambda side: lon_arrival(now, side).wait_recv())
         if t >= 1:
@@ -214,10 +241,16 @@
                 return carry
 
             lax.fori_loop(0, piece, one_column, 0)
-            each_side(has_lat, lambda side: lat_copy(later, side, c).start())
+            @pl.when(c < whole_pieces)
+            def _():
+                each_side(has_lat, lambda side: lat_copy(later, side, c).start())
+
             return carry
 
         lax.fori_loop(0, pieces, one_piece, 0)
+        if t == STEPS - 2:
+            for k in range(tiles):
+                each_side(has_lat, lambda side: tile_copy(later, side, k).start())
         each_side(has_lev, lambda side: lev_copy(later, side).start())
         each_side(has_lon, lambda side: lon_copy(later, side).start())
 
@@ -225,75 +258,108 @@
     each_side(has_lev, lambda side: lev_arrival(now, side).wait_recv())
     each_side(has_lon, lambda side: lon_arrival(now, side).wait_recv())
 
-    def last_columns(y, start, count):
+    def open_row(y):
+        sums[y, 0] = advance(now, y, 0)
+        sums[y, 1] = jnp.zeros((depth, members), jnp.float32)
+        sums[y, 2] = jnp.zeros((depth, members), jnp.float32)
+
+    def last_columns(y, start, count, z=slice(None)):
+        shift = sums[y, 0, z]
+
         def one_column(i, carry):
-            out_ref[y, start + i] = advance(now, y, start + i)
-            return carry
-
-        lax.fori_loop(0, count, one_column, 0)
-
-    def stat_copy(y, k):
-        return pltpu.make_async_remote_copy(
-            src_ref=stat_in.at[0, y],
-            dst_ref=stat_in.at[k, y],
-            send_sem=stat_send.at[y, k],
-            recv_sem=stat_recv.at[y, k],
-            device_id={"lon": lax.rem(lon + k, lons)},
+            total, square = carry
+            value = advance(now, y, start + i, z)
+            out_ref[y, start + i, z] = value
+            moved = value - shift
+            return total + moved, square + moved * moved
+
+        total, square = lax.fori_loop(0, count, one_column, (sums[y, 1, z], sums[y, 2, z]))
+        sums[y, 1, z] = total
+        sums[y, 2, z] = square
+
+    def levels_of(k):
+        return slice(k * tile, (k + 1) * tile)
+
+    def stat_copy(y, k, hop):
+        return pltpu.make_async_remote_copy(
+            src_ref=stat_in.at[0, y, k],
+            dst_ref=stat_in.at[hop, y, k],
+            send_sem=stat_send.at[y, k, hop],
+            recv_sem=stat_recv.at[y, k, hop],
+            device_id={"lon": lax.rem(lon + hop, lons)},
             device_id_type=MESH,
         )
 
-    def send_stats(y):
-        zero = jnp.zeros((depth, members), jnp.float32)
-        mean = lax.fori_loop(0, width, lambda x, s: s + out_ref[y, x], zero) / width
-
-        def square(x, s):
-            d = out_ref[y, x] - mean
-            return s + d * d
-
-        stat_in[0, y, 0] = mean
-        stat_in[0, y, 1] = lax.fori_loop(0, width, square, zero)
-        for k in range(1, lons):
-            stat_copy(y, k).start()
-
-    def take_stats(y):
-        for k in range(1, lons):
-            stat_copy(y, k).wait()
-        means = [stat_in[k, y, 0] for k in range(lons)]
+    def send_stats(y, k):
+        z = levels_of(k)
+        total = sums[y, 1, z]
+        stat_in[0, y, k, 0] = sums[y, 0, z] + total / width
+        stat_in[0, y, k, 1] = jnp.maximum(sums[y, 2, z] - total * (total / width), 0.0)
+        for hop in range(1, lons):
+            stat_copy(y, k, hop).start()
+
+    def take_stats(y, k):
+        z = levels_of(k)
+        for hop in range(1, lons):
+            stat_copy(y, k, hop).wait()
+        means = [stat_in[hop, y, k, 0] for hop in range(lons)]
         mean = functools.reduce(jnp.add, means) / lons
-        squares = functools.reduce(jnp.add, [stat_in[k, y, 1] for k in range(lons)])
+        squares = functools.reduce(jnp.add, [stat_in[hop, y, k, 1] for hop in range(lons)])
         apart = functools.reduce(jnp.add, [(m - mean) * (m - mean) for m in means])
         variance = squares / (width * lons) + apart / lons
-        stat_ref[y, 0] = mean
-        stat_ref[y, 1] = lax.rsqrt(variance + EPS)
+        stat_ref[y, 0, z] = mean
+        stat_ref[y, 1, z] = lax.rsqrt(variance + EPS)
+
+    def edge_row(side):
+        return 0 if side == 0 else rows - 1
 
     low = has_lat[0].astype(jnp.int32)
     high = rows - has_lat[1].astype(jnp.int32)
 
     def free_row(y, carry):
+        open_row(y)
         last_columns(y, 0, width)
-        send_stats(y)
+        for k in range(tiles):
+            send_stats(y, k)
         return carry
 
     lax.fori_loop(low, high, free_row, 0)
+
+    def sent_before(c, carry):
+        each_side(has_lat, lambda side: lat_copy(later, side, c).wait_send())
+        return carry
 
     def last_piece(c, carry):
         def finish(side):
             lat_arrival(now, side, c).wait_recv()
-            lat_copy(later, side, c).wait_send()
-            last_columns(0 if side == 0 else rows - 1, c * piece, piece)
+
+            @pl.when(c == 0)
+            def _():
+                open_row(edge_row(side))
+
+            last_columns(edge_row(side), c * piece, piece)
 
         each_side(has_lat, finish)
         return carry
 
-    lax.fori_loop(0, pieces, last_piece, 0)
-    each_side(has_lat, lambda side: send_stats(0 if side == 0 else rows - 1))
+    lax.fori_loop(0, head, last_piece, 0)
 
     def take(y, carry):
-        take_stats(y)
+        for k in range(tiles):
+            take_stats(y, k)
         return carry
 
     lax.fori_loop(low, high, take, 0)
-    each_side(has_lat, lambda side: take_stats(0 if side == 0 else rows - 1))
+    lax.fori_loop(0, pieces, sent_before, 0)
+    for k in range(tiles):
+        def finish_tile(side):
+            tile_arrival(now, side, k).wait_recv()
+            last_columns(edge_row(side), head * piece, width - head * piece, levels_of(k))
+            send_stats(edge_row(side), k)
+
+        each_side(has_lat, finish_tile)
+    for k in range(tiles):
+        each_side(has_lat, lambda side: take_stats(edge_row(side), k))
 
     for parity in (0, 1):
         each_side(has_lev, lambda side: lev_copy(parity, side).wait_send())
@@ -303,7 +369,9 @@
         each_side(has_lat, lambda side: lat_copy(now, side, c).wait_send())
         return carry
 
-    lax.fori_loop(0, pieces, drain, 0)
+    lax.fori_loop(0, head, drain, 0)
+    for k in range(tiles):
+        each_side(has_lat, lambda side: tile_copy(now, side, k).wait_send())
 
 
 def finish_kernel(state_ref, stat_ref, norm_hbm, temp_hbm, staged, norm_sem, temp_sem):
@@ -330,6 +398,7 @@
     def shards(initial_state, scaled_wind_north, scaled_wind_east, scaled_wind_upward):
         rows, width, depth, members = initial_state.shape
         pieces = pieces_of(width)
+        tiles = depth // 8 if depth % 8 == 0 else 1
         f32 = jnp.float32
         dma = pltpu.SemaphoreType.DMA
         anywhere = pl.BlockSpec(memory_space=pl.ANY)
@@ -347,16 +416,19 @@
                 pltpu.VMEM((3, rows, width, depth, members), f32),
                 pltpu.VMEM((2, 2, rows, width, 1, members), f32),
                 pltpu.VMEM((2, 2, rows, width, 1, members), f32),
-                pltpu.VMEM((lons, rows, 2, depth, members), f32),
+                pltpu.VMEM((lons, rows, tiles, 2, depth // tiles, members), f32),
+                pltpu.VMEM((rows, 3, depth, members), f32),
                 dma((4,)),
                 dma((2, 2, pieces)),
                 dma((2, 2, pieces)),
+                dma((2, tiles)),
+                dma((2, tiles)),
                 dma((2, 2)),
                 dma((2, 2)),
                 dma((2, 2)),
                 dma((2, 2)),
-                dma((rows, lons)),
-                dma((rows, lons)),
+                dma((rows, tiles, lons)),
+                dma((rows, tiles, lons)),
             ],
             compiler_params=pltpu.CompilerParams(
                 collective_id=0, has_side_effects=True, vmem_limit_bytes=44 * MIB

time: 152 us -> 151 us (level)
  no operation moved by 1% of the time
where the time goes in v2:
time: 151 us
  Pallas kernels  150 us (99%)
    pallas_call x1, Pallas kernels, shards(): pl.pallas_call(functools.partial(march_kernel, pieces), out_shape=(pltpu....  146 us
    pallas_call x1, Pallas kernels, shards(): pl.pallas_call(finish_kernel, out_shape=(jax.ShapeDtypeStruct((rows, widt...  4.68 us

profile of v2, /device:TPU:0, one launch (start us, length us, event | category | flops | bytes accessed | tf_op | source)
XLA Modules:
  0.0 151.0 jit_solution(11210764458535448072)
XLA Ops:
  0.6 145.6 %march.1 = (f32[4,96,32,128]{3,2,1,0:T(8,128)S(1)}, f32[4,2,32,128]{3,2,1,0:T(8,128)S(1)}) custom-call(f32[4,96,32,128]{3,2,1,0:T(8,128)} %state_hbm.1, f32[4,96,32,128]{3,2,1,0:T(8,128)} %north_hbm.1, f32[4,96,32,128]{3,2,1,0:T(8,128)} %east_hbm.1, f32[4,96,32,128]{3,2,1,0:T(8,128)} %up_hbm.1), custom_call_target="tpu_custom_call" | custom-call | tf_op jit(solution)/shard_map/march/pallas_call | solution.py:406
  146.3 4.7 %finish.1 = (f32[4,96,32,128]{3,2,1,0:T(8,128)}, f32[4,96,32,128]{3,2,1,0:T(8,128)}) custom-call(f32[4,96,32,128]{3,2,1,0:T(8,128)S(1)} %get-tuple-element.4.state_ref, f32[4,2,32,128]{3,2,1,0:T(8,128)S(1)} %get-tuple-element.5.stat_ref), custom_call_target="tpu_custom_call" | custom-call | tf_op jit(solution)/shard_map/finish/pallas_call | solution.py:438
